TPU v7x, 32 devices: a whole 2x2x4 slice. The times are simulated.
32 devices in a mesh: tm: 8 (over z, y), mp: 4 (over x, core).
Axes of the slice: x: 2, y: 2, z: 4, core: 2. Of those that a mesh axis runs over, the one named last changes fastest.
Arguments:
- latents: float32 [4, 8, 4, 4096], P(None, 'tm'), may hold values from -6 to 6
- noise: float32 [4, 8, 4, 4096], P(None, 'tm'), may hold values from -6 to 6
- start_step: int32 [4], replicated, may hold values from 8 to 999
- slide: int32 [4], replicated, may hold values from 1 to 8, as said below
- w_in: float32 [4, 320], replicated, may hold values from -3 to 3
- w_gate: bfloat16 [320, 1280], P(None, 'mp'), may hold values from -0.3125 to 0.3125
- w_value: bfloat16 [320, 1280], P(None, 'mp'), may hold values from -0.3125 to 0.3125
- w_down: bfloat16 [1280, 320], P('mp'), may hold values from -0.15625 to 0.15625
- w_out: float32 [320, 4], replicated, may hold values from -0.3125 to 0.3125
Outputs:
- next_window: float32 [4, 8, 4, 4096], P(None, 'tm')
- eps: float32 [4, 8, 4, 4096], P(None, 'tm', None, 'mp')
Inputs may be any that keep to these rules, and one draw needn't show every extreme that they name: `slide`: some prompt slides by exactly 8, and another by exactly 1.
All inputs are finite; a program needn't handle non-finite values.
Results may differ from a plain program's by a relative error of at most 0.0023.
Values sent between devices are 32-bit elements; how exact they have to be, the bound alone decides.
No kernel may reach another device: no remote copies, remote signals or barrier semaphores. Data moves between devices by JAX's collectives and lax.ppermute only.
A program may use at most 64 MiB of HBM per device.

v0:
```python
import math

import jax
import jax.numpy as jnp
from jax import lax
from jax.sharding import PartitionSpec as P

TSTEPS = 1000


def prefix(x, axis, combine, identity):
    peers, mine = (lax.axis_size(axis), lax.axis_index(axis))
    everything = lax.all_gather(x, axis)
    start = jnp.broadcast_to(jnp.asarray(identity, x.dtype), x.shape)

    def lap(k, before):
        reached = k < mine
        new = combine(before, everything[k])
        return jnp.where(reached, new, before)

    return lax.fori_loop(0, peers, lap, start)


def from_root(block, axis, holder):
    block = jnp.where(lax.axis_index(axis) == holder, block, jnp.zeros_like(block))
    return lax.psum(block, axis)


def from_behind(block, axis, distance):
    devices = range(lax.axis_size(axis))
    route = [(i - distance, i) for i in devices if i - distance in devices]
    return lax.ppermute(block, axis, route)


def plan(count):
    steps_f = jnp.arange(count, dtype=jnp.float32)
    beta = 0.0001 + (0.02 - 0.0001) * steps_f / (count - 1)
    abar = jnp.cumprod(1.0 - beta)
    return (beta, abar)


def lookup(table, times):
    grid = jnp.arange(table.shape[0], dtype=jnp.int32)
    return jnp.sum(jnp.where(times[..., None] == grid, table, 0.0), axis=-1)


def embed(times, channels):
    half = channels // 2
    freq = jnp.exp(-math.log(10000.0) * jnp.arange(half, dtype=jnp.float32) / half)
    angle = times[..., None] * freq
    return jnp.concatenate([jnp.cos(angle), jnp.sin(angle)], axis=-1)


def add_terms(earlier, later):
    return earlier + later


def shards(latents, noise, start_step, slide, w_in, w_gate, w_value, w_down, w_out):
    prompts, t_dev, lat, pos = latents.shape
    channels = w_in.shape[1]
    n_tm = lax.axis_size("tm")
    window = n_tm * t_dev
    share_width = pos // lax.axis_size("mp")
    share_offset = lax.axis_index("mp") * share_width
    slots = lax.axis_index("tm") * t_dev + jnp.arange(t_dev, dtype=jnp.int32)
    times = start_step[:, None] - slots[None, :]
    beta, abar = plan(TSTEPS)
    beta_t = lookup(beta, times)[:, :, None, None]
    abar_t = lookup(abar, times)[:, :, None, None]
    vectors = embed(times.astype(jnp.float32), channels).reshape(prompts * t_dev, channels)
    folded = jnp.dot(w_down.astype(jnp.float32), w_out, precision=lax.Precision.HIGHEST)
    items = latents.reshape(prompts * t_dev, lat, pos)

    def denoise(pair):
        latent, vector = pair
        hid = jnp.dot(w_in.T, latent, precision=lax.Precision.HIGHEST) + vector[:, None]
        mean = jnp.mean(hid, axis=0)
        var = jnp.mean((hid - mean) ** 2, axis=0)
        normed = ((hid - mean) * lax.rsqrt(var + 1e-05)).astype(jnp.bfloat16)
        gate = jnp.einsum("cf,cp->fp", w_gate, normed, preferred_element_type=jnp.float32)
        value = jnp.einsum("cf,cp->fp", w_value, normed, preferred_element_type=jnp.float32)
        hidden = (jax.nn.gelu(gate, approximate=False) * value).astype(jnp.bfloat16)
        partial_eps = jnp.dot(folded.T, hidden, precision=lax.Precision.HIGHEST)
        base_eps = jnp.dot(w_out.T, hid, precision=lax.Precision.HIGHEST)
        return (partial_eps, base_eps)

    partials, bases = lax.map(denoise, (items, vectors))
    eps = lax.psum(partials, "mp") + bases
    eps = eps.reshape(prompts, t_dev, lat, pos)
    eps_share = lax.dynamic_slice_in_dim(eps, share_offset, share_width, 3)
    stepped = (latents - beta_t / jnp.sqrt(1.0 - abar_t) * eps) / jnp.sqrt(1.0 - beta_t) + jnp.sqrt(
        beta_t
    ) * noise
    drift = stepped - latents
    first = (slots == 0)[None, :, None, None]
    head_part = jnp.where(first, latents, 0.0)
    terms = drift + head_part
    totals = jnp.sum(terms, axis=1)
    before = prefix(totals, "tm", add_terms, jnp.zeros_like(totals))
    updated = before[:, None] + (jnp.cumsum(terms, axis=1) - terms) + head_part
    last = from_root(updated[:, -1], "tm", n_tm - 1)
    moved = updated
    for bit in range((window // 2).bit_length()):
        step = 1 << bit
        incoming = from_behind(moved, "tm", -max(1, step // t_dev))
        taken = slide >> bit & 1 == 1
        moved = jnp.where(taken[:, None, None, None], incoming, moved)
    beyond = slots[None, :] + slide[:, None] >= window
    result = jnp.where(beyond[:, :, None, None], last[:, None], moved)
    return (result, eps_share)


def solution(mesh):
    in_specs = (
        P(None, "tm", None, None),
        P(None, "tm", None, None),
        P(),
        P(),
        P(),
        P(None, "mp"),
        P(None, "mp"),
        P("mp", None),
        P(),
    )
    out_specs = (P(None, "tm", None, None), P(None, "tm", None, "mp"))
    return jax.shard_map(shards, mesh=mesh, in_specs=in_specs, out_specs=out_specs, check_vma=False)
```

profile of v0, /device:TPU:0, one launch (start us, length us, event | category | flops | bytes accessed | tf_op | source)
XLA Modules:
  0.0 305.6 jit_solution(13553774158699933047)
XLA Ops:
  9.6 99.3 %while.26 = (s32[]{:T(128)}, f32[4,4,4096]{2,1,0:T(4,128)S(1)}, f32[4,4,4096]{2,1,0:T(4,128)S(1)}, f32[4,4,4096]{2,1,0:T(4,128)}, f32[4,320]{1,0:T(4,128)}, /*in...) while((s32[]{:T(128)}, f32[4,4,4096]{2,1,0:T(4,128)S(1)}, ...), condition=%wide.region_7.8_spmd, body=%wide.region_4.7_spmd.sunk | while | flops 1967394816 | bytes 44411340 | solution.py:87
  9.7 5.4 %fusion.60 = (f32[4096]{0:T(1024)S(1)}, f32[4096,320]{0,1:T(8,128)S(1)}) fusion(f32[320]{0:T(512)S(1)} %dynamic-slice_reduce_fusion.2, f32[4,320]{1,0:T(4,128)} %get-tuple-element.315, f32[4,4,4096]{2,1,0:T(4,128)} %get-tuple-element.314, s32[]{:T(128)} %get-tuple-element.300), kind=kOutput, calls=%fused_computation.72.clone.1 | convolution fusion | flops 65531904 | bytes 5332736 | tf_op jit(solution)/shard_map/while/body/eval_jaxpr/dot_general | solution.py:76
  15.7 1.6 fusion.61
  17.3 13.1 %fusion.62 = bf16[320,4096]{1,0:T(8,128)(2,1)S(1)} fusion(bf16[320,320]{1,0:T(8,128)(2,1)S(1)} %copy-done.8, f32[4096,320]{0,1:T(8,128)S(1)} %fusion.61, f32[4096,320]{0,1:T(8,128)S(1)} %get-tuple-element.283, f32[4096]{0:T(1024)S(1)} %add_rsqrt_fusion.2, f32[4096]{0:T(1024)S(1)} %broadcast_multiply_fusion.2), kind=kOutput, calls=%fused_computation.5.clone.1 | convolution fusion | flops 929300480 | bytes 13344768 | tf_op jit(solution)/shard_map/while/body/eval_jaxpr/cf,cp->fp/dot_general | solution.py:81
  31.6 2.8 fusion.64
  34.5 5.3 %fusion.60 = (f32[4096]{0:T(1024)S(1)}, f32[4096,320]{0,1:T(8,128)S(1)}) fusion(f32[320]{0:T(512)S(1)} %dynamic-slice_reduce_fusion.2, f32[4,320]{1,0:T(4,128)} %get-tuple-element.315, f32[4,4,4096]{2,1,0:T(4,128)} %get-tuple-element.314, s32[]{:T(128)} %get-tuple-element.300), kind=kOutput, calls=%fused_computation.72.clone.1 | convolution fusion | flops 65531904 | bytes 5332736 | tf_op jit(solution)/shard_map/while/body/eval_jaxpr/dot_general | solution.py:76
  40.5 1.6 fusion.61
  42.2 13.1 %fusion.62 = bf16[320,4096]{1,0:T(8,128)(2,1)S(1)} fusion(bf16[320,320]{1,0:T(8,128)(2,1)S(1)} %copy-done.8, f32[4096,320]{0,1:T(8,128)S(1)} %fusion.61, f32[4096,320]{0,1:T(8,128)S(1)} %get-tuple-element.283, f32[4096]{0:T(1024)S(1)} %add_rsqrt_fusion.2, f32[4096]{0:T(1024)S(1)} %broadcast_multiply_fusion.2), kind=kOutput, calls=%fused_computation.5.clone.1 | convolution fusion | flops 929300480 | bytes 13344768 | tf_op jit(solution)/shard_map/while/body/eval_jaxpr/cf,cp->fp/dot_general | solution.py:81
  56.5 2.8 fusion.64
  59.3 5.3 %fusion.60 = (f32[4096]{0:T(1024)S(1)}, f32[4096,320]{0,1:T(8,128)S(1)}) fusion(f32[320]{0:T(512)S(1)} %dynamic-slice_reduce_fusion.2, f32[4,320]{1,0:T(4,128)} %get-tuple-element.315, f32[4,4,4096]{2,1,0:T(4,128)} %get-tuple-element.314, s32[]{:T(128)} %get-tuple-element.300), kind=kOutput, calls=%fused_computation.72.clone.1 | convolution fusion | flops 65531904 | bytes 5332736 | tf_op jit(solution)/shard_map/while/body/eval_jaxpr/dot_general | solution.py:76
  67.0 13.1 %fusion.62 = bf16[320,4096]{1,0:T(8,128)(2,1)S(1)} fusion(bf16[320,320]{1,0:T(8,128)(2,1)S(1)} %copy-done.8, f32[4096,320]{0,1:T(8,128)S(1)} %fusion.61, f32[4096,320]{0,1:T(8,128)S(1)} %get-tuple-element.283, f32[4096]{0:T(1024)S(1)} %add_rsqrt_fusion.2, f32[4096]{0:T(1024)S(1)} %broadcast_multiply_fusion.2), kind=kOutput, calls=%fused_computation.5.clone.1 | convolution fusion | flops 929300480 | bytes 13344768 | tf_op jit(solution)/shard_map/while/body/eval_jaxpr/cf,cp->fp/dot_general | solution.py:81
  81.3 2.8 fusion.64
  84.1 5.3 %fusion.60 = (f32[4096]{0:T(1024)S(1)}, f32[4096,320]{0,1:T(8,128)S(1)}) fusion(f32[320]{0:T(512)S(1)} %dynamic-slice_reduce_fusion.2, f32[4,320]{1,0:T(4,128)} %get-tuple-element.315, f32[4,4,4096]{2,1,0:T(4,128)} %get-tuple-element.314, s32[]{:T(128)} %get-tuple-element.300), kind=kOutput, calls=%fused_computation.72.clone.1 | convolution fusion | flops 65531904 | bytes 5332736 | tf_op jit(solution)/shard_map/while/body/eval_jaxpr/dot_general | solution.py:76
  91.8 13.1 %fusion.62 = bf16[320,4096]{1,0:T(8,128)(2,1)S(1)} fusion(bf16[320,320]{1,0:T(8,128)(2,1)S(1)} %copy-done.8, f32[4096,320]{0,1:T(8,128)S(1)} %fusion.61, f32[4096,320]{0,1:T(8,128)S(1)} %get-tuple-element.283, f32[4096]{0:T(1024)S(1)} %add_rsqrt_fusion.2, f32[4096]{0:T(1024)S(1)} %broadcast_multiply_fusion.2), kind=kOutput, calls=%fused_computation.5.clone.1 | convolution fusion | flops 929300480 | bytes 13344768 | tf_op jit(solution)/shard_map/while/body/eval_jaxpr/cf,cp->fp/dot_general | solution.py:81
  106.1 2.8 fusion.64
  110.5 34.3 %all-reduce.4.cloned.1.call-done = f32[4,4,4096]{2,1,0:T(4,128)} async-done(((f32[4,4,4096]{2,1,0:T(4,128)}), f32[4,4,4096]{2,1,0:T(4,128)}) %all-reduce.4.cloned.1.call-update) | async-done | bytes 262160 | tf_op jit(solution)/shard_map/psum | solution.py:88
  144.8 1.9 fusion.26
  146.8 49.8 %all-gather.3.cloned.1.call-done = f32[32,1,4,4096]{3,2,1,0:T(4,128)} async-done(((f32[4,1,4,4096]{3,2,1,0:T(4,128)}), f32[32,1,4,4096]{3,2,1,0:T(4,128)}) %all-gather.3.cloned.1.call-update) | async-done | bytes 2097168 | tf_op jit(solution)/shard_map/all_gather | solution.py:13
  196.6 10.1 %while.27 = (s32[]{:T(128)}, f32[4,4,4096]{2,1,0:T(4,128)S(1)}, s32[]{:T(128)}, f32[8,4,4,4096]{3,2,1,0:T(4,128)}, s32[]{:T(128)}, /*index=5*/s32[]{:T(128)}) while((s32[]{:T(128)}, f32[4,4,4096]{2,1,0:T(4,128)S(1)}, s32[]{:T(128)}, f32[8,4,4,4096]{3,2,1,0:T(4,128)}, s32[]{:T(128)}, /*index=5*/s32[]{:T(128)}) %tuple.75), condition=%wide.region_10.11_spmd.clone, body=%wide.region_9.10_spmd.clone.sunk | while | flops 196612 | bytes 786525 | solution.py:21
  206.7 1.8 broadcast_select_fusion
  209.8 6.9 %collective-permute-done = f32[4,1,4,4096]{3,2,1,0:T(4,128)S(1)} collective-permute-done((f32[4,1,4,4096]{3,2,1,0:T(4,128)S(1)}, f32[4,1,4,4096]{3,2,1,0:T(4,128)S(1)}, u32[]{:S(2)}, u32[]{:S(2)}) %collective-permute-start) | collective-permute-done | bytes 262176 | tf_op jit(solution)/shard_map/ppermute | solution.py:32
  218.2 7.1 %collective-permute-done.1 = f32[4,1,4,4096]{3,2,1,0:T(4,128)S(1)} collective-permute-done((f32[4,1,4,4096]{3,2,1,0:T(4,128)S(1)}, f32[4,1,4,4096]{3,2,1,0:T(4,128)S(1)}, u32[]{:S(2)}, u32[]{:S(2)}) %collective-permute-start.1) | collective-permute-done | bytes 262176 | tf_op jit(solution)/shard_map/ppermute | solution.py:32
  227.4 69.9 %all-reduce.6.cloned.1.call-done = f32[4,1,4,4096]{3,2,1,0:T(4,128)} async-done(((f32[4,1,4,4096]{3,2,1,0:T(4,128)}), f32[4,1,4,4096]{3,2,1,0:T(4,128)}) %all-reduce.6.cloned.1.call-update) | async-done | bytes 262160 | tf_op jit(solution)/shard_map/psum | solution.py:26
  297.2 1.8 select_select_fusion
  (98 shorter events, 29.1 us)
Async XLA Ops:
  7.2 1.5 copy-start
  7.2 137.6 %all-reduce.4.cloned.1.call-start = ((), (), s32[]{:S(2)}) async-start(), calls=%async_computation | async-start | bytes 524288 | tf_op jit(solution)/shard_map/psum | solution.py:88
  9.6 100.7 %copy-start.6 = (s32[4]{0:T(128)S(1)}, s32[4]{0:T(128)}, u32[]{:S(2)}) copy-start(s32[4]{0:T(128)} %get-tuple-element.187) | copy-start | bytes 52
  9.6 135.2 %copy-start.4 = (f32[4,1,4,4096]{3,2,1,0:T(4,128)S(1)}, f32[4,1,4,4096]{3,2,1,0:T(4,128)}, u32[]{:S(2)}) copy-start(f32[4,1,4,4096]{3,2,1,0:T(4,128)} %param.14) | copy-start | bytes 786436
  9.7 6.0 %copy-start.1 = (bf16[320,320]{1,0:T(8,128)(2,1)S(1)}, bf16[320,320]{1,0:T(8,128)(2,1)}, u32[]{:S(2)}) copy-start(bf16[320,320]{1,0:T(8,128)(2,1)} %get-tuple-element.317) | copy-start | bytes 614404 | tf_op jit(solution)/shard_map/while
  15.7 1.6 copy-start.8
  17.3 14.3 %copy-start.5 = (f32[320,4]{0,1:T(4,128)S(1)}, f32[320,4]{0,1:T(4,128)}, u32[]{:S(2)}) copy-start(f32[320,4]{0,1:T(4,128)} %get-tuple-element.320) | copy-start | bytes 15364 | tf_op jit(solution)/shard_map/while
  34.5 6.0 %copy-start.1 = (bf16[320,320]{1,0:T(8,128)(2,1)S(1)}, bf16[320,320]{1,0:T(8,128)(2,1)}, u32[]{:S(2)}) copy-start(bf16[320,320]{1,0:T(8,128)(2,1)} %get-tuple-element.317) | copy-start | bytes 614404 | tf_op jit(solution)/shard_map/while
  40.5 1.6 copy-start.8
  42.1 14.3 %copy-start.5 = (f32[320,4]{0,1:T(4,128)S(1)}, f32[320,4]{0,1:T(4,128)}, u32[]{:S(2)}) copy-start(f32[320,4]{0,1:T(4,128)} %get-tuple-element.320) | copy-start | bytes 15364 | tf_op jit(solution)/shard_map/while
  59.3 6.0 %copy-start.1 = (bf16[320,320]{1,0:T(8,128)(2,1)S(1)}, bf16[320,320]{1,0:T(8,128)(2,1)}, u32[]{:S(2)}) copy-start(bf16[320,320]{1,0:T(8,128)(2,1)} %get-tuple-element.317) | copy-start | bytes 614404 | tf_op jit(solution)/shard_map/while
  65.3 1.6 copy-start.8
  67.0 14.3 %copy-start.5 = (f32[320,4]{0,1:T(4,128)S(1)}, f32[320,4]{0,1:T(4,128)}, u32[]{:S(2)}) copy-start(f32[320,4]{0,1:T(4,128)} %get-tuple-element.320) | copy-start | bytes 15364 | tf_op jit(solution)/shard_map/while
  84.1 6.0 %copy-start.1 = (bf16[320,320]{1,0:T(8,128)(2,1)S(1)}, bf16[320,320]{1,0:T(8,128)(2,1)}, u32[]{:S(2)}) copy-start(bf16[320,320]{1,0:T(8,128)(2,1)} %get-tuple-element.317) | copy-start | bytes 614404 | tf_op jit(solution)/shard_map/while
  90.1 1.6 copy-start.8
  91.8 14.3 %copy-start.5 = (f32[320,4]{0,1:T(4,128)S(1)}, f32[320,4]{0,1:T(4,128)}, u32[]{:S(2)}) copy-start(f32[320,4]{0,1:T(4,128)} %get-tuple-element.320) | copy-start | bytes 15364 | tf_op jit(solution)/shard_map/while
  108.9 0.7 copy-start.3
  108.9 97.8 %copy-start.2 = (f32[4,4,4096]{2,1,0:T(4,128)S(1)}, f32[4,4,4096]{2,1,0:T(4,128)}, u32[]{:S(2)}) copy-start(f32[4,4,4096]{2,1,0:T(4,128)} %get-tuple-element.343) | copy-start | bytes 786436
  108.9 100.8 %copy-start.7 = (s32[4]{0:T(128)S(1)}, s32[4]{0:T(128)}, u32[]{:S(2)}) copy-start(s32[4]{0:T(128)} %param.16) | copy-start | bytes 52
  109.6 87.0 %all-gather.3.cloned.1.call-start = ((), (), s32[]{:S(2)}) async-start(), calls=%async_computation.2 | async-start | bytes 2359296 | tf_op jit(solution)/shard_map/all_gather | solution.py:13
  146.8 150.5 %all-reduce.6.cloned.1.call-start = ((), (), s32[]{:S(2)}) async-start(), calls=%async_computation.1 | async-start | bytes 524288 | tf_op jit(solution)/shard_map/psum | solution.py:26
  208.5 8.3 %collective-permute-start = (f32[4,1,4,4096]{3,2,1,0:T(4,128)S(1)}, f32[4,1,4,4096]{3,2,1,0:T(4,128)S(1)}, u32[]{:S(2)}, u32[]{:S(2)}) collective-permute-start(f32[4,1,4,4096]{3,2,1,0:T(4,128)S(1)} %get-tuple-element.183), channel_id=1, source_target_pairs={{4,0},{8,4},{12,8},{16,12},{20,16},{24,20},{28,24},{5,1},{9,5},{13... | collective-permute-start | bytes 786440 | tf_op jit(solution)/shard_map/ppermute | solution.py:32
  216.9 8.4 %collective-permute-start.1 = (f32[4,1,4,4096]{3,2,1,0:T(4,128)S(1)}, f32[4,1,4,4096]{3,2,1,0:T(4,128)S(1)}, u32[]{:S(2)}, u32[]{:S(2)}) collective-permute-start(f32[4,1,4,4096]{3,2,1,0:T(4,128)S(1)} %broadcast_select_fusion.1), channel_id=1, source_target_pairs={{8,0},{12,4},{16,8},{20,12},{24,16},{28,20},{9,1},{13,5},{17,9},{2... | collective-permute-start | bytes 786440 | tf_op jit(solution)/shard_map/ppermute | solution.py:32
  225.4 71.8 %collective-permute-start.2 = (f32[4,1,4,4096]{3,2,1,0:T(4,128)S(1)}, f32[4,1,4,4096]{3,2,1,0:T(4,128)S(1)}, u32[]{:S(2)}, u32[]{:S(2)}) collective-permute-start(f32[4,1,4,4096]{3,2,1,0:T(4,128)S(1)} %broadcast_select_fusion.2), channel_id=1, source_target_pairs={{16,0},{20,4},{24,8},{28,12},{17,1},{21,5},{25,9},{29,13},{18,2},{... | collective-permute-start | bytes 786440 | tf_op jit(solution)/shard_map/ppermute | solution.py:32
Sparse Core Ops, SparseCore 0:
  109.8 34.9 all-reduce.3
  147.5 49.0 all-gather.2
  218.3 78.8 all-reduce.5
where the time goes:
time: 306 us
  waiting for transfers between devices  168 us (55%)
  matrix products  97.2 us (32%)
  other arithmetic  20.2 us (7%)
  between operations  13.9 us (5%)
  starting transfers between devices  3.99 us (1%)
    psum x1, waiting for transfers between devices, from_root(): return lax.psum(block, axis)  69.9 us
    dot_general x4, matrix products, denoise(): jnp.einsum('cf,cp->fp', w_value, normed, preferred_element_type=jnp.float32)  52.5 us
    all_gather x1, waiting for transfers between devices, prefix(): everything = lax.all_gather(x, axis)  49.8 us
    psum x1, waiting for transfers between devices, shards(): eps = lax.psum(partials, 'mp') + bases  34.3 us
    dot_general x4, matrix products, denoise(): jnp.dot(w_in.T, latent, precision=lax.Precision.HIGHEST) + vector[:, None]  21.4 us
    ppermute x3, waiting for transfers between devices, from_behind(): return lax.ppermute(block, axis, route)  14 us
    dot_general x4, matrix products, denoise(): base_eps = jnp.dot(w_out.T, hid, precision=lax.Precision.HIGHEST)  11.3 us
    select_n x8, other arithmetic, lap(): return jnp.where(reached, new, before)  9.92 us
  transfers between devices with their start and end apart: 6, of which 5 were waited for; matrix products, arithmetic and copies ran while one was open for 1% of the time, Pallas kernels for 0%

commit v1 on v0

v1 whole, which is shorter than its diff:
```python
import math

import jax
import jax.numpy as jnp
import numpy as np
from jax import lax
from jax.experimental import pallas as pl
from jax.experimental.pallas import tpu as pltpu
from jax.sharding import PartitionSpec as P

TSTEPS = 1000
GROUPS = 6
TILE = 256
F32 = jnp.float32
BF16 = jnp.bfloat16


def plan_table(count):
    beta = 0.0001 + (0.02 - 0.0001) * np.arange(count, dtype=np.float64) / (count - 1)
    abar = np.cumprod(1.0 - beta)
    table = np.stack([beta / np.sqrt(1.0 - abar), 1.0 / np.sqrt(1.0 - beta), np.sqrt(beta)])
    return jnp.asarray(table.astype(np.float32))


def split3(x):
    high = x.astype(BF16).astype(F32)
    rest = x - high
    mid = rest.astype(BF16).astype(F32)
    return high, mid, rest - mid


def radices(count):
    found = []
    while count > 1:
        if count % 4 == 0 and (count.bit_length() - 1) % 2 == 0:
            radix = 4
        elif count % 2 == 0:
            radix = 2
        else:
            radix = count
        found.append(radix)
        count //= radix
    return found


def prep(start, slot, w_in, w_gate, w_value, w_down, w_out_t):
    lat, channels = w_in.shape
    prompts = start.shape[0]
    hidden = w_gate.shape[1]
    rows = lat + prompts
    half = channels // 2

    def body(start_ref, slot_ref, in_ref, gate_ref, value_ref, down_ref, out_ref, pack_ref, table_ref):
        lane = lax.broadcasted_iota(jnp.int32, (prompts, channels), 1)
        item = lax.broadcasted_iota(jnp.int32, (prompts, channels), 0)
        first_half = lane < half
        k = jnp.where(first_half, lane, lane - half).astype(F32)
        freq = jnp.exp(k * (-math.log(10000.0)) / half)
        times = jnp.zeros((prompts, channels), F32)
        for p in range(prompts):
            times = jnp.where(item == p, (start_ref[p] - slot_ref[0]).astype(F32), times)
        angle = times * freq
        emb = jnp.where(first_half, jnp.cos(angle), jnp.sin(angle))
        raw = jnp.concatenate([in_ref[...], emb], axis=0)
        centred = raw - jnp.sum(raw, axis=1, keepdims=True) * (1.0 / channels)
        place = lax.broadcasted_iota(jnp.int32, (rows, 128), 1)
        row_id = lax.broadcasted_iota(jnp.int32, (rows, 1), 0)
        table = jnp.zeros((rows, 128), F32)
        scale = channels ** -0.5
        rest = centred
        for s in range(lat):
            pivot = rest[s:s + 1]
            square = jnp.sum(pivot * pivot, axis=1, keepdims=True)
            pivot = pivot * jnp.where(square > 0, lax.rsqrt(square), 0.0)
            along = jnp.sum(rest * pivot, axis=1, keepdims=True)
            along = jnp.where(row_id >= s, along, 0.0)
            table = jnp.where(place == s, along * scale, table)
            rest = rest - along * pivot
        left = jnp.sqrt(jnp.sum(rest * rest, axis=1, keepdims=True))
        table = jnp.where(place == lat, left * scale, table)
        out_t = out_ref[...]
        for l in range(lat):
            base = jnp.sum(raw * out_t[l:l + 1], axis=1, keepdims=True)
            table = jnp.where(place == lat + 1 + l, base, table)
        table_ref[...] = table
        parts = jnp.concatenate(split3(centred), axis=0).astype(BF16)
        for i, weight_ref in enumerate((gate_ref, value_ref)):
            got = jnp.dot(parts, weight_ref[...], preferred_element_type=F32)
            got = got[:rows] + got[rows:2 * rows] + got[2 * rows:]
            pack_ref[i * rows:(i + 1) * rows] = got * math.sqrt(0.5)
        zero = jnp.zeros((rows - lat, channels), F32)
        wide = [jnp.concatenate([part, zero], axis=0) for part in split3(out_t)]
        parts = jnp.concatenate(wide, axis=0).astype(BF16)
        got = lax.dot_general(parts, down_ref[...], (((1,), (1,)), ((), ())), preferred_element_type=F32)
        pack_ref[2 * rows:] = got[:rows] + got[rows:2 * rows] + got[2 * rows:]

    smem = pl.BlockSpec(memory_space=pltpu.SMEM)
    vmem = pl.BlockSpec(memory_space=pltpu.VMEM)
    return pl.pallas_call(
        body,
        out_shape=(jax.ShapeDtypeStruct((3 * rows, hidden), F32), jax.ShapeDtypeStruct((rows, 128), F32)),
        in_specs=[smem, smem] + [vmem] * 5,
        out_specs=(vmem, vmem),
        name="prep",
    )(start, slot, w_in, w_gate, w_value, w_down, w_out_t)


def denoise(place, table, coef, latents, noise, packs):
    prompts, _, lat, pos = latents.shape
    peers, _, hidden = packs.shape
    rows = lat + prompts
    share = pos // peers
    tile = min(TILE, share)

    def body(place_ref, table_ref, coef_ref, lat_ref, noise_ref, pack_ref, term_ref, eps_ref, gate_lhs, value_lhs, fold_lhs):
        p = pl.program_id(0)

        @pl.when(p == 0)
        def _():
            for s in range(peers):
                for i, dest in enumerate((gate_lhs, value_lhs)):
                    high, mid, low = split3(pack_ref[s, i * rows:(i + 1) * rows])
                    stacked = jnp.concatenate([high, high, mid, high, low, mid], axis=0)
                    dest[s] = jnp.transpose(stacked).astype(BF16)
                high, mid, low = split3(pack_ref[s, 2 * rows:])
                pair = high + jnp.concatenate([mid[rows - lat:], mid[:rows - lat]], axis=0)
                fold_lhs[s] = jnp.concatenate([pair, low], axis=0).astype(BF16)

        mine = [lat_ref[0, 0, c:c + 1, :] for c in range(lat)]
        var = jnp.zeros((1, share), F32)
        for s in range(lat + 1):
            line = jnp.zeros((1, share), F32) + table_ref[lat + p, s]
            for c in range(s, lat):
                line = line + table_ref[c, s] * mine[c]
            var = var + line * line
        rstd = lax.rsqrt(var + 1e-05)
        lines = lax.broadcasted_iota(jnp.int32, (rows, share), 0)
        scaled = jnp.where(lines == lat + p, 1.0, 0.0)
        for c in range(lat):
            scaled = jnp.where(lines == c, mine[c], scaled)
        high, mid, low = split3(scaled * rstd)
        rhs = jnp.concatenate([high, mid, high, low, high, mid], axis=0).astype(BF16)
        outs = []
        for n in range(share // tile):
            cut = rhs[:, n * tile:(n + 1) * tile]
            total = jnp.zeros((2 * rows, tile), F32)
            for s in range(peers):
                gate = jnp.dot(gate_lhs[s], cut, preferred_element_type=F32)
                value = jnp.dot(value_lhs[s], cut, preferred_element_type=F32)
                act = (gate * value * (1.0 + lax.erf(gate))).astype(BF16)
                total = total + jnp.dot(fold_lhs[s], act, preferred_element_type=F32)
            outs.append(total[:lat] + total[rows - lat:rows] + total[rows:rows + lat])
        branch = jnp.concatenate(outs, axis=1)
        for l in range(lat):
            base = jnp.zeros((1, share), F32) + table_ref[lat + p, lat + 1 + l]
            for c in range(lat):
                base = base + table_ref[c, lat + 1 + l] * mine[c]
            eps = branch[l:l + 1] + base
            eps_ref[0, 0, l:l + 1, :] = eps
            stepped = (mine[l] - coef_ref[p, 0] * eps) * coef_ref[p, 1] + coef_ref[p, 2] * noise_ref[0, 0, l:l + 1, :]
            head = jnp.where(place_ref[1] == 0, mine[l], 0.0)
            term_ref[0, l:l + 1, :] = stepped - mine[l] + head

    smem = pl.BlockSpec(memory_space=pltpu.SMEM)
    grid_spec = pltpu.PrefetchScalarGridSpec(
        num_scalar_prefetch=1,
        grid=(prompts,),
        in_specs=[
            smem,
            smem,
            pl.BlockSpec((1, 1, lat, share), lambda p, place: (p, 0, 0, place[0])),
            pl.BlockSpec((1, 1, lat, share), lambda p, place: (p, 0, 0, place[0])),
            pl.BlockSpec(packs.shape, lambda p, place: (0, 0, 0)),
        ],
        out_specs=[
            pl.BlockSpec((1, lat, share), lambda p, place: (p, 0, 0)),
            pl.BlockSpec((1, 1, lat, share), lambda p, place: (p, 0, 0, 0)),
        ],
        scratch_shapes=[
            pltpu.VMEM((peers, hidden, GROUPS * rows), BF16),
            pltpu.VMEM((peers, hidden, GROUPS * rows), BF16),
            pltpu.VMEM((peers, 2 * rows, hidden), BF16),
        ],
    )
    return pl.pallas_call(
        body,
        grid_spec=grid_spec,
        out_shape=[
            jax.ShapeDtypeStruct((prompts, lat, share), F32),
            jax.ShapeDtypeStruct((prompts, 1, lat, share), F32),
        ],
        name="denoise",
    )(place, table, coef, latents, noise, packs)


def slid_sums(term, slide, axis):
    count = lax.axis_size(axis)
    mine = lax.axis_index(axis)

    def wanted(target, source):
        reach = jnp.minimum(target + slide, count - 1)
        return (source < reach)[:, None, None]

    digits = radices(count)
    below = 1
    held = None
    for radix in digits:
        digit = mine // below % radix

        def peer(i, k):
            d = i // below % radix
            return i + ((d + k) % radix - d) * below

        above = count // (below * radix)
        last_place = mine % (below * radix)
        if held is None:
            raws, sources = [term], [mine]
            for k in range(1, radix):
                raws.append(lax.ppermute(term, axis, [(i, peer(i, k)) for i in range(count)]))
                sources.append(peer(mine, radix - k))

            def partial(target):
                parts = [jnp.where(wanted(target, s), r, 0.0) for r, s in zip(raws, sources)]
                return sum(parts[1:], parts[0])

            held = partial
        else:
            earlier = held
            place = mine % below

            def offer(k):
                d = (digit + k) % radix
                return jnp.stack([earlier(place + d * below + a * below * radix) for a in range(above)])

            got = offer(0)
            for k in range(1, radix):
                got = got + lax.ppermute(offer(k), axis, [(i, peer(i, k)) for i in range(count)])

            def chosen(target, got=got, span=below * radix):
                if got.shape[0] == 1:
                    return got[0]
                return lax.dynamic_index_in_dim(got, target // span, 0, keepdims=False)

            held = chosen
        below *= radix
    if held is None:
        return jnp.where(wanted(mine, mine), term, 0.0)
    return held(mine)


def shards(latents, noise, start_step, slide, w_in, w_gate, w_value, w_down, w_out):
    prompts, t_dev, lat, pos = latents.shape
    assert t_dev == 1
    slot = lax.axis_index("tm").astype(jnp.int32)
    member = lax.axis_index("mp").astype(jnp.int32)
    pack, table = prep(start_step, slot[None], w_in, w_gate, w_value, w_down, w_out.T)
    packs = lax.all_gather(pack, "mp")
    plan = plan_table(TSTEPS)
    grid = jnp.arange(TSTEPS, dtype=jnp.int32)
    hit = (start_step - slot)[:, None, None] == grid
    coef = jnp.sum(jnp.where(hit, plan[None], 0.0), axis=-1)
    term, eps = denoise(jnp.stack([member, slot]), table, coef, latents, noise, packs)
    share = slid_sums(term, slide, "tm")
    result = lax.all_gather(share, "mp", axis=2, tiled=True)
    return result[:, None], eps


def solution(mesh):
    in_specs = (
        P(None, "tm", None, None),
        P(None, "tm", None, None),
        P(),
        P(),
        P(),
        P(None, "mp"),
        P(None, "mp"),
        P("mp", None),
        P(),
    )
    out_specs = (P(None, "tm", None, None), P(None, "tm", None, "mp"))
    return jax.shard_map(shards, mesh=mesh, in_specs=in_specs, out_specs=out_specs, check_vma=False)
```

time: 306 us -> 50.7 us (0.17)
  waiting for transfers between devices: 168 us -> 7.67 us
  matrix products: 97.2 us -> 0 us
  other arithmetic: 20.2 us -> 1.01 us
  Pallas kernels: 0 us -> 17.9 us
  blocking collectives: 0 us -> 14.2 us
  between operations: 13.9 us -> 0.68 us
    psum x2 -> x0, waiting for transfers between devices: 104 us -> none  [the longest x1 69.9 us: from_root(): return lax.psum(block, axis)]
    dot_general x21 -> x0, matrix products: 97.2 us -> none  [the longest x4 52.5 us: denoise(): jnp.einsum('cf,cp->fp', w_value, normed, preferred_element_type=jnp.float32)]
    all_gather x1 -> x0, waiting for transfers between devices: 49.8 us -> none  [prefix(): everything = lax.all_gather(x, axis)]
    pallas_call x0 -> x2, Pallas kernels: none -> 17.9 us  [the longest x1 15.2 us: denoise(): pl.pallas_call(body, grid_spec=grid_spec, out_shape=[jax.ShapeDtypeStruct...]
    all_gather x0 -> x2, blocking collectives: none -> 14.2 us  [the longest x1 8.43 us: shards(): packs = lax.all_gather(pack, 'mp')]
    select_n x12 -> x0, other arithmetic: 13.8 us -> none  [the longest x8 9.92 us: lap(): return jnp.where(reached, new, before)]
    ppermute x3 -> x4, waiting for transfers between devices: 14 us -> 7.67 us  [the longest x3 5.34 us: slid_sums(): lax.ppermute(offer(k), axis, [(i, peer(i, k)) for i in range(count)])]
    ppermute x3 -> x4, starting transfers between devices: 3.86 us -> 6.17 us  [the longest x3 4.66 us: slid_sums(): lax.ppermute(offer(k), axis, [(i, peer(i, k)) for i in range(count)])]
  transfers between devices with their start and end apart: 6 -> 4, of which waited for: 5 -> 3; matrix products, arithmetic and copies ran while one was open for 1% -> 0% of each run, Pallas kernels for 0% -> 0%
where the time goes in v1:
time: 50.7 us; the launch traced here: 50.4 us
  Pallas kernels  17.9 us (35%)
  blocking collectives  14.2 us (28%)
  waiting for transfers between devices  7.67 us (15%)
  starting transfers between devices  6.17 us (12%)
  local copies, waits for them, and re-layouts  2.73 us (5%)
  other arithmetic  1.01 us (2%)
  between operations  0.68 us (1%)
    pallas_call x1, Pallas kernels, denoise(): pl.pallas_call(body, grid_spec=grid_spec, out_shape=[jax.ShapeDtypeStruct...  15.2 us
    all_gather x1, blocking collectives, shards(): packs = lax.all_gather(pack, 'mp')  8.43 us
    all_gather x1, blocking collectives, shards(): result = lax.all_gather(share, 'mp', axis=2, tiled=True)  5.78 us
    ppermute x3, waiting for transfers between devices, slid_sums(): lax.ppermute(offer(k), axis, [(i, peer(i, k)) for i in range(count)])  5.34 us
    ppermute x3, starting transfers between devices, slid_sums(): lax.ppermute(offer(k), axis, [(i, peer(i, k)) for i in range(count)])  4.66 us
    pallas_call x1, Pallas kernels, prep(): pl.pallas_call(body, out_shape=(jax.ShapeDtypeStruct((3 * rows, hidden),...  2.73 us
    ppermute x1, waiting for transfers between devices, slid_sums(): lax.ppermute(term, axis, [(i, peer(i, k)) for i in range(count)])  2.33 us
    unnamed x9, local copies, waits for them, and re-layouts  2.05 us
  transfers between devices with their start and end apart: 4, of which 3 were waited for; matrix products, arithmetic and copies ran while one was open for 0% of the time, Pallas kernels for 0%

profile of v1, /device:TPU:0, one launch (start us, length us, event | category | flops | bytes accessed | tf_op | source)
XLA Modules:
  0.0 50.4 jit_solution(17050670540850149885)
XLA Ops:
  0.6 0.0 copy-start.1
  0.6 0.0 copy-start.3
  0.7 0.6 %copy-done.3 = s32[4]{0:T(128)S(1)} copy-done((s32[4]{0:T(128)S(1)}, s32[4]{0:T(128)}, u32[]{:S(2)}) %copy-start.3) | copy-done | bytes 40
  1.3 0.1 iota_compare_fusion
  1.4 0.0 copy-done.1
  1.4 0.1 select_reduce_fusion
  1.5 0.7 %copy.13.coef_ref = f32[4,3]{1,0:T(4,128)} copy(f32[4,3]{0,1:T(4,128)S(1)} %select_reduce_fusion) | data formatting | bytes 96 | tf_op jit(solution)/shard_map/reduce_sum | solution.py:261
  2.2 0.6 %pad_add_fusion.place_ref = s32[2]{0:T(128)} fusion(s32[1]{0:T(128)} %bitcast.1.slot_ref, s32[1]{0:T(128)} %bitcast), kind=kLoop, calls=%fused_computation.8 | loop fusion | flops 2 | bytes 16 | tf_op jit(solution)/shard_map/stack | solution.py:262
  2.8 2.7 %prep.1 = (f32[24,320]{1,0:T(8,128)}, f32[8,128]{1,0:T(8,128)}) custom-call(s32[4]{0:T(128)} %start_ref.1, s32[1]{0:T(128)} %bitcast.1.slot_ref, f32[4,320]{1,0:T(4,128)} %in_ref.1, bf16[320,320]{1,0:T(8,128)(2,1)} %gate_ref.1, bf16[320,320]{1,0:T(8,128)(2,1)} %value_ref.1, bf16[320,320]{1,0:T(8,128)(2,1)} %down_ref.1, f32[4,320]{1,0:T(4,128)} %bitcast.21), custom_call_target="tpu_custom_call" | custom-call | tf_op jit(solution)/shard_map/prep/pallas_call | solution.py:99
  5.5 8.4 %all-gather = f32[96,320]{1,0:T(8,128)} all-gather(f32[24,320]{1,0:T(8,128)} %get-tuple-element.7), channel_id=2, replica_groups=mesh['tm'=8,'mp'=4] {'mp'}, dimensions={0}, use_global_device_ids=true | all-gather | bytes 153600 | tf_op jit(solution)/shard_map/all_gather | solution.py:257
  13.9 15.2 %denoise.1 = (f32[4,4,1024]{2,1,0:T(4,128)}, f32[4,1,4,1024]{3,2,1,0:T(4,128)}) custom-call(s32[2]{0:T(128)} %pad_add_fusion.place_ref, f32[8,128]{1,0:T(8,128)} %get-tuple-element.6.table_ref, f32[4,3]{1,0:T(4,128)} %copy.13.coef_ref, f32[4,1,4,4096]{3,2,1,0:T(4,128)} %lat_ref.1, f32[4,1,4,4096]{3,2,1,0:T(4,128)} %noise_ref.1, f32[4,24,320]{2,1,0:T(8,128)} %bitcast.20), custom_call_target="tpu_custom_call" | custom-call | tf_op jit(solution)/shard_map/denoise/pallas_call | solution.py:185
  29.1 1.5 %collective-permute-start = (f32[4,4,1024]{2,1,0:T(4,128)}, f32[4,4,1024]{2,1,0:T(4,128)S(1)}, u32[]{:S(2)}, u32[]{:S(2)}) collective-permute-start(f32[4,4,1024]{2,1,0:T(4,128)} %get-tuple-element.8), channel_id=1, source_target_pairs={{0,4},{4,0},{8,12},{12,8},{16,20},{20,16},{24,28},{28,24},{1,5},{5... | collective-permute-start | bytes 196616 | tf_op jit(solution)/shard_map/ppermute | solution.py:219
  30.6 0.7 %copy-done.2 = s32[4]{0:T(128)S(1)} copy-done((s32[4]{0:T(128)S(1)}, s32[4]{0:T(128)}, u32[]{:S(2)}) %copy-start.2) | copy-done | bytes 40
  31.3 2.3 %collective-permute-done = f32[4,4,1024]{2,1,0:T(4,128)S(1)} collective-permute-done((f32[4,4,1024]{2,1,0:T(4,128)}, f32[4,4,1024]{2,1,0:T(4,128)S(1)}, u32[]{:S(2)}, u32[]{:S(2)}) %collective-permute-start) | collective-permute-done | bytes 65568 | tf_op jit(solution)/shard_map/ppermute | solution.py:219
  33.6 0.1 add_bitcast_fusion.2
  33.8 1.6 %collective-permute-start.1 = (f32[1,4,4,1024]{3,2,1,0:T(4,128)S(1)}, f32[1,4,4,1024]{3,2,1,0:T(4,128)S(1)}, u32[]{:S(2)}, u32[]{:S(2)}) collective-permute-start(f32[1,4,4,1024]{3,2,1,0:T(4,128)S(1)} %get-tuple-element.14), channel_id=1, source_target_pairs={{0,8},{4,12},{8,16},{12,20},{16,24},{20,28},{24,0},{28,4},{1,9},{5... | collective-permute-start | bytes 196616 | tf_op jit(solution)/shard_map/ppermute | solution.py:237
  35.4 2.2 %collective-permute-start.3 = (f32[1,4,4,1024]{3,2,1,0:T(4,128)S(1)}, f32[1,4,4,1024]{3,2,1,0:T(4,128)S(1)}, u32[]{:S(2)}, u32[]{:S(2)}) collective-permute-start(f32[1,4,4,1024]{3,2,1,0:T(4,128)S(1)} %get-tuple-element.15), channel_id=1, source_target_pairs={{0,24},{4,28},{8,0},{12,4},{16,8},{20,12},{24,16},{28,20},{1,25},{... | collective-permute-start | bytes 196616 | tf_op jit(solution)/shard_map/ppermute | solution.py:237
  37.6 0.8 %collective-permute-start.2 = (f32[1,4,4,1024]{3,2,1,0:T(4,128)S(1)}, f32[1,4,4,1024]{3,2,1,0:T(4,128)S(1)}, u32[]{:S(2)}, u32[]{:S(2)}) collective-permute-start(f32[1,4,4,1024]{3,2,1,0:T(4,128)S(1)} %get-tuple-element.16), channel_id=1, source_target_pairs={{0,16},{4,20},{8,24},{12,28},{16,0},{20,4},{24,8},{28,12},{1,17},{... | collective-permute-start | bytes 196616 | tf_op jit(solution)/shard_map/ppermute | solution.py:237
  38.4 2.1 %collective-permute-done.1 = f32[1,4,4,1024]{3,2,1,0:T(4,128)S(1)} collective-permute-done((f32[1,4,4,1024]{3,2,1,0:T(4,128)S(1)}, f32[1,4,4,1024]{3,2,1,0:T(4,128)S(1)}, u32[]{:S(2)}, u32[]{:S(2)}) %collective-permute-start.1) | collective-permute-done | bytes 65568 | tf_op jit(solution)/shard_map/ppermute | solution.py:237
  40.6 0.0 collective-permute-done.3
  40.6 3.2 %collective-permute-done.2 = f32[1,4,4,1024]{3,2,1,0:T(4,128)S(1)} collective-permute-done((f32[1,4,4,1024]{3,2,1,0:T(4,128)S(1)}, f32[1,4,4,1024]{3,2,1,0:T(4,128)S(1)}, u32[]{:S(2)}, u32[]{:S(2)}) %collective-permute-start.2) | collective-permute-done | bytes 65568 | tf_op jit(solution)/shard_map/ppermute | solution.py:237
  43.8 0.1 fusion.1
  43.9 5.8 %all-gather.1 = f32[1,4,4,4096]{3,2,1,0:T(4,128)S(1)} all-gather(f32[1,4,4,1024]{3,2,1,0:T(4,128)S(1)} %fusion.1), channel_id=3, replica_groups=mesh['tm'=8,'mp'=4] {'mp'}, dimensions={3}, use_global_device_ids=true | all-gather | bytes 327680 | tf_op jit(solution)/shard_map/all_gather | solution.py:264
  49.7 0.7 %copy.16 = f32[4,1,4,4096]{3,2,1,0:T(4,128)} copy(f32[4,1,4,4096]{3,2,1,0:T(4,128)S(1)} %bitcast.19) | data formatting | bytes 524288
  (5 shorter events, 0.0 us)
Async XLA Ops:
  0.6 0.8 %copy-start.1 = (f32[3,1000]{1,0:T(4,128)S(1)}, f32[3,1000]{1,0:T(4,128)}, u32[]{:S(2)}) copy-start(f32[3,1000]{1,0:T(4,128)} %constant.83.clone) | copy-start | bytes 36004
  0.6 0.7 %copy-start.3 = (s32[4]{0:T(128)S(1)}, s32[4]{0:T(128)}, u32[]{:S(2)}) copy-start(s32[4]{0:T(128)} %start_ref.1) | copy-start | bytes 52
  29.1 4.5 %collective-permute-start = (f32[4,4,1024]{2,1,0:T(4,128)}, f32[4,4,1024]{2,1,0:T(4,128)S(1)}, u32[]{:S(2)}, u32[]{:S(2)}) collective-permute-start(f32[4,4,1024]{2,1,0:T(4,128)} %get-tuple-element.8), channel_id=1, source_target_pairs={{0,4},{4,0},{8,12},{12,8},{16,20},{20,16},{24,28},{28,24},{1,5},{5... | collective-permute-start | bytes 196616 | tf_op jit(solution)/shard_map/ppermute | solution.py:219
  30.6 3.0 %copy-start = (f32[4,4,1024]{2,1,0:T(4,128)S(1)}, f32[4,4,1024]{2,1,0:T(4,128)}, u32[]{:S(2)}) copy-start(f32[4,4,1024]{2,1,0:T(4,128)} %get-tuple-element.8) | copy-start | bytes 196612
  30.6 0.7 %copy-start.2 = (s32[4]{0:T(128)S(1)}, s32[4]{0:T(128)}, u32[]{:S(2)}) copy-start(s32[4]{0:T(128)} %param.13) | copy-start | bytes 52
  33.8 6.8 %collective-permute-start.1 = (f32[1,4,4,1024]{3,2,1,0:T(4,128)S(1)}, f32[1,4,4,1024]{3,2,1,0:T(4,128)S(1)}, u32[]{:S(2)}, u32[]{:S(2)}) collective-permute-start(f32[1,4,4,1024]{3,2,1,0:T(4,128)S(1)} %get-tuple-element.14), channel_id=1, source_target_pairs={{0,8},{4,12},{8,16},{12,20},{16,24},{20,28},{24,0},{28,4},{1,9},{5... | collective-permute-start | bytes 196616 | tf_op jit(solution)/shard_map/ppermute | solution.py:237
  35.4 5.2 %collective-permute-start.3 = (f32[1,4,4,1024]{3,2,1,0:T(4,128)S(1)}, f32[1,4,4,1024]{3,2,1,0:T(4,128)S(1)}, u32[]{:S(2)}, u32[]{:S(2)}) collective-permute-start(f32[1,4,4,1024]{3,2,1,0:T(4,128)S(1)} %get-tuple-element.15), channel_id=1, source_target_pairs={{0,24},{4,28},{8,0},{12,4},{16,8},{20,12},{24,16},{28,20},{1,25},{... | collective-permute-start | bytes 196616 | tf_op jit(solution)/shard_map/ppermute | solution.py:237
  37.6 6.1 %collective-permute-start.2 = (f32[1,4,4,1024]{3,2,1,0:T(4,128)S(1)}, f32[1,4,4,1024]{3,2,1,0:T(4,128)S(1)}, u32[]{:S(2)}, u32[]{:S(2)}) collective-permute-start(f32[1,4,4,1024]{3,2,1,0:T(4,128)S(1)} %get-tuple-element.16), channel_id=1, source_target_pairs={{0,16},{4,20},{8,24},{12,28},{16,0},{20,4},{24,8},{28,12},{1,17},{... | collective-permute-start | bytes 196616 | tf_op jit(solution)/shard_map/ppermute | solution.py:237

commit v2 on v1

v2 whole, which is shorter than its diff:
```python
import math

import jax
import jax.numpy as jnp
import numpy as np
from jax import lax
from jax.experimental import pallas as pl
from jax.experimental.pallas import tpu as pltpu
from jax.sharding import PartitionSpec as P

TSTEPS = 1000
GROUPS = 6
VMEM_BYTES = 24 * 2**20
F32 = jnp.float32
BF16 = jnp.bfloat16


def plan_table(count):
    beta = 0.0001 + (0.02 - 0.0001) * np.arange(count, dtype=np.float64) / (count - 1)
    abar = np.cumprod(1.0 - beta)
    table = np.stack([beta / np.sqrt(1.0 - abar), 1.0 / np.sqrt(1.0 - beta), np.sqrt(beta)])
    wide = -count % 128
    return jnp.asarray(np.pad(table, ((0, 5), (0, wide))).astype(np.float32))


def split3(x):
    high = x.astype(BF16).astype(F32)
    rest = x - high
    mid = rest.astype(BF16).astype(F32)
    return high, mid, rest - mid


def radices(count):
    found = []
    while count > 1:
        if count % 4 == 0 and (count.bit_length() - 1) % 2 == 0:
            radix = 4
        elif count % 2 == 0:
            radix = 2
        else:
            radix = count
        found.append(radix)
        count //= radix
    return found


def params():
    return pltpu.CompilerParams(vmem_limit_bytes=VMEM_BYTES)


def cost(units):
    return pl.CostEstimate(flops=300 * units, transcendentals=units, bytes_accessed=0)


def project(start, slot, member, w_in, w_out_t, w_gate, w_value, w_down, latents, noise, share):
    lat, channels = w_in.shape
    prompts = start.shape[0]
    hidden = w_gate.shape[1]
    rows = lat + prompts
    half = channels // 2

    def body(start_ref, slot_ref, member_ref, in_ref, out_ref, *refs):
        gate_hbm, value_hbm, down_hbm, lat_hbm, noise_hbm = refs[:5]
        pack_ref, raw_ref, lat_ref, noise_ref, gate_ref, value_ref, down_ref, sems = refs[5:]
        cut = pl.ds(member_ref[0] * share, share)
        moves = [
            (gate_hbm, gate_ref),
            (value_hbm, value_ref),
            (down_hbm, down_ref),
            (lat_hbm.at[:, 0, :, cut], lat_ref),
            (noise_hbm.at[:, 0, :, cut], noise_ref),
        ]
        copies = [pltpu.make_async_copy(src, dst, sems.at[i]) for i, (src, dst) in enumerate(moves)]
        for copy in copies:
            copy.start()
        lane = lax.broadcasted_iota(jnp.int32, (prompts, channels), 1)
        item = lax.broadcasted_iota(jnp.int32, (prompts, channels), 0)
        first_half = lane < half
        k = jnp.where(first_half, lane, lane - half).astype(F32)
        freq = jnp.exp(k * (-math.log(10000.0)) / half)
        times = jnp.zeros((prompts, channels), F32)
        for p in range(prompts):
            times = jnp.where(item == p, (start_ref[p] - slot_ref[0]).astype(F32), times)
        angle = times * freq
        emb = jnp.where(first_half, jnp.cos(angle), jnp.sin(angle))
        raw = jnp.concatenate([in_ref[...], emb], axis=0)
        raw_ref[...] = raw
        centred = raw - jnp.sum(raw, axis=1, keepdims=True) * (1.0 / channels)
        parts = jnp.concatenate(split3(centred), axis=0).astype(BF16)
        for i, weight_ref in enumerate((gate_ref, value_ref)):
            copies[i].wait()
            got = jnp.dot(parts, weight_ref[...], preferred_element_type=F32)
            got = got[:rows] + got[rows:2 * rows] + got[2 * rows:]
            pack_ref[i * rows:(i + 1) * rows] = got * math.sqrt(0.5)
        zero = jnp.zeros((rows - lat, channels), F32)
        wide = [jnp.concatenate([part, zero], axis=0) for part in split3(out_ref[...])]
        parts = jnp.concatenate(wide, axis=0).astype(BF16)
        copies[2].wait()
        got = lax.dot_general(parts, down_ref[...], (((1,), (1,)), ((), ())), preferred_element_type=F32)
        pack_ref[2 * rows:] = got[:rows] + got[rows:2 * rows] + got[2 * rows:]
        for copy in copies[3:]:
            copy.wait()

    smem = pl.BlockSpec(memory_space=pltpu.SMEM)
    vmem = pl.BlockSpec(memory_space=pltpu.VMEM)
    hbm = pl.BlockSpec(memory_space=pltpu.HBM)
    return pl.pallas_call(
        body,
        out_shape=(
            jax.ShapeDtypeStruct((3 * rows, hidden), F32),
            jax.ShapeDtypeStruct((rows, channels), F32),
            jax.ShapeDtypeStruct((prompts, lat, share), F32),
            jax.ShapeDtypeStruct((prompts, lat, share), F32),
        ),
        in_specs=[smem] * 3 + [vmem] * 2 + [hbm] * 5,
        out_specs=(vmem,) * 4,
        scratch_shapes=[
            pltpu.VMEM(w_gate.shape, BF16),
            pltpu.VMEM(w_value.shape, BF16),
            pltpu.VMEM(w_down.shape, BF16),
            pltpu.SemaphoreType.DMA((5,)),
        ],
        compiler_params=params(),
        name="project",
    )(start, slot, member, w_in, w_out_t, *[pltpu.with_memory_space_constraint(x, pltpu.HBM) for x in (w_gate, w_value, w_down, latents, noise)])


def load_lhs(pack_ref, s, gate_lhs, value_lhs, fold_lhs, lat):
    rows = pack_ref.shape[1] // 3
    for i, dest in enumerate((gate_lhs, value_lhs)):
        high, mid, low = split3(pack_ref[s, i * rows:(i + 1) * rows])
        stacked = jnp.concatenate([high, high, mid, high, low, mid], axis=0)
        dest[s] = jnp.transpose(stacked).astype(BF16)
    high, mid, low = split3(pack_ref[s, 2 * rows:])
    pair = high + jnp.concatenate([mid[rows - lat:], mid[:rows - lat]], axis=0)
    fold_lhs[s] = jnp.concatenate([pair, low], axis=0).astype(BF16)


def hidden_sum(rhs, peers, gate_lhs, value_lhs, fold_lhs, lat):
    total = None
    for s in range(peers):
        gate = jnp.dot(gate_lhs[s], rhs, preferred_element_type=F32)
        value = jnp.dot(value_lhs[s], rhs, preferred_element_type=F32)
        act = (gate * value * (1.0 + lax.erf(gate))).astype(BF16)
        got = jnp.dot(fold_lhs[s], act, preferred_element_type=F32)
        total = got if total is None else total + got
    rows = total.shape[0] // 2
    return total[:lat] + total[rows - lat:rows] + total[rows:rows + lat]


def lhs_scratch(peers, rows, hidden):
    return [
        pltpu.VMEM((peers, hidden, GROUPS * rows), BF16),
        pltpu.VMEM((peers, hidden, GROUPS * rows), BF16),
        pltpu.VMEM((peers, 2 * rows, hidden), BF16),
    ]


def begin(start, slot, raw, w_out_t, plan, latents, packs):
    prompts, lat, share = latents.shape
    rows, channels = raw.shape
    peers, _, hidden = packs.shape

    def body(start_ref, slot_ref, raw_ref, out_ref, plan_ref, lat_ref, pack_ref, rhs_ref, eps_ref, coef_ref, gate_lhs, value_lhs, fold_lhs):
        for s in range(peers):
            load_lhs(pack_ref, s, gate_lhs, value_lhs, fold_lhs, lat)
        raw_rows = raw_ref[...]
        scale = channels ** -0.5
        rest = raw_rows - jnp.sum(raw_rows, axis=1, keepdims=True) * (1.0 / channels)
        row_id = lax.broadcasted_iota(jnp.int32, (rows, 1), 0)
        upper = []
        for s in range(lat):
            pivot = rest[s:s + 1]
            along = jnp.sum(rest * pivot, axis=1, keepdims=True)
            square = along[s:s + 1]
            inverse = jnp.where(square > 0, lax.rsqrt(square), 0.0)
            along = jnp.where(row_id >= s, along * inverse, 0.0)
            upper.append(along * scale)
            rest = rest - along * (pivot * inverse)
        left = jnp.sqrt(jnp.sum(rest * rest, axis=1, keepdims=True)) * scale
        out_t = out_ref[...]
        base = [jnp.sum(out_t * raw_rows[r:r + 1], axis=1, keepdims=True) for r in range(rows)]
        place = lax.broadcasted_iota(jnp.int32, plan_ref.shape, 1)
        lines = lax.broadcasted_iota(jnp.int32, (rows, share), 0)
        for p in range(prompts):
            hit = place == start_ref[p] - slot_ref[0]
            found = jnp.sum(jnp.where(hit, plan_ref[...], 0.0), axis=1, keepdims=True)
            coef_ref[p] = jnp.broadcast_to(found, coef_ref.shape[1:])
            mine = [lat_ref[p, c:c + 1, :] for c in range(lat)]
            var = left[lat + p:lat + p + 1] * left[lat + p:lat + p + 1]
            for s in range(lat):
                line = upper[s][lat + p:lat + p + 1]
                for c in range(s, lat):
                    line = line + upper[s][c:c + 1] * mine[c]
                var = var + line * line
            rstd = lax.rsqrt(var + 1e-05)
            scaled = jnp.where(lines == lat + p, 1.0, 0.0)
            for c in range(lat):
                scaled = jnp.where(lines == c, mine[c], scaled)
            high, mid, low = split3(scaled * rstd)
            rhs = jnp.concatenate([high, mid, high, low, high, mid], axis=0).astype(BF16)
            rhs_ref[p] = rhs
            eps = base[lat + p] + hidden_sum(rhs, peers, gate_lhs, value_lhs, fold_lhs, lat)
            for c in range(lat):
                eps = eps + base[c] * mine[c]
            eps_ref[p] = eps

    smem = pl.BlockSpec(memory_space=pltpu.SMEM)
    vmem = pl.BlockSpec(memory_space=pltpu.VMEM)
    return pl.pallas_call(
        body,
        out_shape=(
            jax.ShapeDtypeStruct((prompts, GROUPS * rows, share), BF16),
            jax.ShapeDtypeStruct((prompts, lat, share), F32),
            jax.ShapeDtypeStruct((prompts, plan.shape[0], 128), F32),
        ),
        in_specs=[smem] * 2 + [vmem] * 5,
        out_specs=(vmem,) * 3,
        scratch_shapes=lhs_scratch(peers, rows, hidden),
        compiler_params=params(),
        cost_estimate=cost(prompts * share * peers * hidden),
        name="begin",
    )(start, slot, raw, w_out_t, plan, latents, packs)


def extend(rhs, eps, packs):
    prompts, lat, share = eps.shape
    peers, rows, hidden = packs.shape

    def body(rhs_ref, eps_ref, pack_ref, out_ref, gate_lhs, value_lhs, fold_lhs):
        for s in range(peers):
            load_lhs(pack_ref, s, gate_lhs, value_lhs, fold_lhs, lat)
        for p in range(prompts):
            out_ref[p] = eps_ref[p] + hidden_sum(rhs_ref[p], peers, gate_lhs, value_lhs, fold_lhs, lat)

    vmem = pl.BlockSpec(memory_space=pltpu.VMEM)
    return pl.pallas_call(
        body,
        out_shape=jax.ShapeDtypeStruct(eps.shape, F32),
        in_specs=[vmem] * 3,
        out_specs=vmem,
        scratch_shapes=lhs_scratch(peers, rows // 3, hidden),
        compiler_params=params(),
        cost_estimate=cost(prompts * share * peers * hidden),
        name="extend",
    )(rhs, eps, packs)


def finish(slot, coef, latents, noise, rhs, eps, packs):
    prompts, lat, share = eps.shape
    peers, rows, hidden = packs.shape

    def body(slot_ref, coef_ref, lat_ref, noise_ref, rhs_ref, eps_ref, pack_ref, term_ref, out_ref, gate_lhs, value_lhs, fold_lhs):
        for s in range(peers):
            load_lhs(pack_ref, s, gate_lhs, value_lhs, fold_lhs, lat)
        for p in range(prompts):
            eps = eps_ref[p]
            if peers:
                eps = eps + hidden_sum(rhs_ref[p], peers, gate_lhs, value_lhs, fold_lhs, lat)
            out_ref[p, 0] = eps
            mine = lat_ref[p]
            weights = [coef_ref[p, i:i + 1, 0:1] for i in range(3)]
            stepped = (mine - weights[0] * eps) * weights[1] + weights[2] * noise_ref[p]
            term_ref[p] = stepped - mine + jnp.where(slot_ref[0] == 0, mine, 0.0)

    smem = pl.BlockSpec(memory_space=pltpu.SMEM)
    vmem = pl.BlockSpec(memory_space=pltpu.VMEM)
    return pl.pallas_call(
        body,
        out_shape=(
            jax.ShapeDtypeStruct(eps.shape, F32),
            jax.ShapeDtypeStruct((prompts, 1, lat, share), F32),
        ),
        in_specs=[smem] + [vmem] * 6,
        out_specs=(vmem,) * 2,
        scratch_shapes=lhs_scratch(peers, rows // 3, hidden),
        compiler_params=params(),
        cost_estimate=cost(prompts * share * peers * hidden),
        name="finish",
    )(slot, coef, latents, noise, rhs, eps, packs)


def slid_sums(term, slide, axis):
    count = lax.axis_size(axis)
    mine = lax.axis_index(axis)

    def wanted(target, source):
        reach = jnp.minimum(target + slide, count - 1)
        return (source < reach)[:, None, None]

    digits = radices(count)
    below = 1
    held = None
    for radix in digits:
        digit = mine // below % radix

        def peer(i, k):
            d = i // below % radix
            return i + ((d + k) % radix - d) * below

        above = count // (below * radix)
        last_place = mine % (below * radix)
        if held is None:
            raws, sources = [term], [mine]
            for k in range(1, radix):
                raws.append(lax.ppermute(term, axis, [(i, peer(i, k)) for i in range(count)]))
                sources.append(peer(mine, radix - k))

            def partial(target):
                parts = [jnp.where(wanted(target, s), r, 0.0) for r, s in zip(raws, sources)]
                return sum(parts[1:], parts[0])

            held = partial
        else:
            earlier = held
            place = mine % below

            def offer(k):
                d = (digit + k) % radix
                return jnp.stack([earlier(place + d * below + a * below * radix) for a in range(above)])

            got = offer(0)
            for k in range(1, radix):
                got = got + lax.ppermute(offer(k), axis, [(i, peer(i, k)) for i in range(count)])

            def chosen(target, got=got, span=below * radix):
                if got.shape[0] == 1:
                    return got[0]
                return lax.dynamic_index_in_dim(got, target // span, 0, keepdims=False)

            held = chosen
        below *= radix
    if held is None:
        return jnp.where(wanted(mine, mine), term, 0.0)
    return held(mine)


def swap(x, axis, step):
    count = lax.axis_size(axis)
    return lax.ppermute(x, axis, [(i, i ^ step) for i in range(count)])


def shards(latents, noise, start_step, slide, w_in, w_gate, w_value, w_down, w_out):
    prompts, t_dev, lat, pos = latents.shape
    assert t_dev == 1
    members = lax.axis_size("mp")
    share = pos // members
    slot = lax.axis_index("tm").astype(jnp.int32)[None]
    member = lax.axis_index("mp").astype(jnp.int32)[None]
    w_out_t = w_out.T
    plan = plan_table(TSTEPS)
    pack, raw, lat_share, noise_share = project(
        start_step, slot, member, w_in, w_out_t, w_gate, w_value, w_down, latents, noise, share
    )
    held = pack[None]
    step = members // 2
    arrived = swap(held, "mp", step) if step else None
    rhs, eps, coef = begin(start_step, slot, raw, w_out_t, plan, lat_share, held)
    while step > 1:
        arrived, rhs, eps = lax.optimization_barrier((arrived, rhs, eps))
        held = jnp.concatenate([held, arrived], axis=0)
        step //= 2
        following = swap(held, "mp", step)
        eps = extend(rhs, eps, arrived)
        arrived = following
    term, eps = finish(slot, coef, lat_share, noise_share, rhs, eps, arrived)
    result = slid_sums(term, slide, "tm")
    result = lax.all_gather(result, "mp", axis=2, tiled=True)
    return result[:, None], eps


def solution(mesh):
    in_specs = (
        P(None, "tm", None, None),
        P(None, "tm", None, None),
        P(),
        P(),
        P(),
        P(None, "mp"),
        P(None, "mp"),
        P("mp", None),
        P(),
    )
    out_specs = (P(None, "tm", None, None), P(None, "tm", None, "mp"))
    return jax.shard_map(shards, mesh=mesh, in_specs=in_specs, out_specs=out_specs, check_vma=False)
```

time: 50.7 us -> 38.1 us (0.75)
  blocking collectives: 14.2 us -> 5.78 us
  Pallas kernels: 17.9 us -> 12.3 us
  starting transfers between devices: 6.17 us -> 9.3 us
  local copies, waits for them, and re-layouts: 2.73 us -> 1.39 us
  other arithmetic: 1.01 us -> 0.24 us
    all_gather x2 -> x1, blocking collectives: 14.2 us -> 5.78 us  [shards(): result = lax.all_gather(result, 'mp', axis=2, tiled=True)]
    pallas_call x2 -> x4, Pallas kernels: 17.9 us -> 12.3 us  [the longest x1 4.66 us: finish(): pl.pallas_call(body, out_shape=(jax.ShapeDtypeStruct(eps.shape, F32), jax...]
    ppermute x0 -> x2, starting transfers between devices: none -> 3.1 us  [swap(): return lax.ppermute(x, axis, [(i, i ^ step) for i in range(count)])]
    reduce_sum x1 -> x0, local copies, waits for them, and re-layouts: 0.68 us -> none  [shards(): coef = jnp.sum(jnp.where(hit, plan[None], 0.0), axis=-1)]
    unnamed x9 -> x11, local copies, waits for them, and re-layouts: 2.05 us -> 1.39 us
    another operation x1 -> x0, other arithmetic: 0.6 us -> none  [shards(): jnp.stack([member, slot])]
    ppermute x1, waiting for transfers between devices: 2.33 us -> 2.85 us  [slid_sums(): lax.ppermute(term, axis, [(i, peer(i, k)) for i in range(count)])]
  transfers between devices with their start and end apart: 4 -> 6, of which waited for: 3 -> 3; matrix products, arithmetic and copies ran while one was open for 0% -> 0% of each run, Pallas kernels for 0% -> 15%
where the time goes in v2:
time: 38.1 us; the launch traced here: 37.8 us
  Pallas kernels  12.3 us (32%)
  starting transfers between devices  9.3 us (24%)
  waiting for transfers between devices  8.04 us (21%)
  blocking collectives  5.78 us (15%)
  local copies, waits for them, and re-layouts  1.39 us (4%)
  between operations  0.84 us (2%)
    all_gather x1, blocking collectives, shards(): result = lax.all_gather(result, 'mp', axis=2, tiled=True)  5.78 us
    ppermute x3, waiting for transfers between devices, slid_sums(): lax.ppermute(offer(k), axis, [(i, peer(i, k)) for i in range(count)])  5.19 us
    ppermute x3, starting transfers between devices, slid_sums(): lax.ppermute(offer(k), axis, [(i, peer(i, k)) for i in range(count)])  4.67 us
    pallas_call x1, Pallas kernels, finish(): pl.pallas_call(body, out_shape=(jax.ShapeDtypeStruct(eps.shape, F32), jax...  4.66 us
    pallas_call x1, Pallas kernels, begin(): pl.pallas_call(body, out_shape=(jax.ShapeDtypeStruct((prompts, GROUPS * r...  3.27 us
    ppermute x2, starting transfers between devices, swap(): return lax.ppermute(x, axis, [(i, i ^ step) for i in range(count)])  3.1 us
    ppermute x1, waiting for transfers between devices, slid_sums(): lax.ppermute(term, axis, [(i, peer(i, k)) for i in range(count)])  2.85 us
    pallas_call x1, Pallas kernels, extend(): pl.pallas_call(body, out_shape=jax.ShapeDtypeStruct(eps.shape, F32), in_s...  2.22 us
  transfers between devices with their start and end apart: 6, of which 3 were waited for; matrix products, arithmetic and copies ran while one was open for 0% of the time, Pallas kernels for 15%

profile of v2, /device:TPU:0, one launch (start us, length us, event | category | flops | bytes accessed | tf_op | source)
XLA Modules:
  0.0 37.8 jit_solution(11951432110524035168)
XLA Ops:
  0.6 0.0 copy-start
  0.7 0.7 %copy-done.1 = f32[320,4]{0,1:T(4,128)S(1)} copy-done((f32[320,4]{0,1:T(4,128)S(1)}, f32[320,4]{0,1:T(4,128)}, u32[]{:S(2)}) %copy-start.1) | copy-done | bytes 5144
  1.3 0.0 copy-done
  1.4 2.1 %project.1 = (f32[24,320]{1,0:T(8,128)S(1)}, f32[8,320]{1,0:T(8,128)S(1)}, f32[4,4,1024]{2,1,0:T(4,128)S(1)}, f32[4,4,1024]{2,1,0:T(4,128)S(1)}) custom-call(s32[4]{0:T(128)S(1)} %copy-done.2, s32[1]{0:T(128)} %bitcast.slot_ref, s32[1]{0:T(128)} %bitcast.1.member_ref, f32[4,320]{1,0:T(4,128)S(1)} %copy-done, f32[4,320]{1,0:T(4,128)S(1)} %bitcast.22, ...), custom_call_target="tpu_custom_call" | custom-call | tf_op jit(solution)/shard_map/project/pallas_call | solution.py:107
  3.5 3.0 %collective-permute-start = (f32[1,24,320]{2,1,0:T(8,128)S(1)}, f32[1,24,320]{2,1,0:T(8,128)S(1)}, u32[]{:S(2)}, u32[]{:S(2)}) collective-permute-start(f32[1,24,320]{2,1,0:T(8,128)S(1)} %bitcast.19), channel_id=1, source_target_pairs={{0,2},{1,3},{2,0},{3,1},{4,6},{5,7},{6,4},{7,5},{8,10},{9,11},{10,... | collective-permute-start | bytes 92168 | tf_op jit(solution)/shard_map/ppermute | solution.py:340
  6.5 0.0 copy-done.3
  6.5 3.3 %begin.1 = (bf16[4,48,1024]{2,1,0:T(8,128)(2,1)S(1)}, f32[4,4,1024]{2,1,0:T(4,128)S(1)}, f32[4,8,128]{2,1,0:T(8,128)S(1)}) custom-call(s32[4]{0:T(128)S(1)} %copy-done.2, s32[1]{0:T(128)} %bitcast.slot_ref, f32[8,320]{1,0:T(8,128)S(1)} %get-tuple-element.14.raw_ref, f32[4,320]{1,0:T(4,128)S(1)} %bitcast.23, f32[8,1024]{1,0:T(8,128)S(1)} %copy-done.3, ...), custom_call_target="tpu_custom_call" | custom-call | flops 393216000 | tf_op jit(solution)/shard_map/begin/pallas_call | solution.py:210
  9.8 0.0 collective-permute-done.pack_ref
  9.8 0.1 collective-permute-start.1
  10.0 2.2 %extend.1.eps_ref = f32[4,4,1024]{2,1,0:T(4,128)S(1)} custom-call(bf16[4,48,1024]{2,1,0:T(8,128)(2,1)S(1)} %get-tuple-element.21.rhs_ref, f32[4,4,1024]{2,1,0:T(4,128)S(1)} %get-tuple-element.22.eps_ref, f32[1,24,320]{2,1,0:T(8,128)S(1)} %collective-permute-done.pack_ref), custom_call_target="tpu_custom_call" | custom-call | flops 393216000 | tf_op jit(solution)/shard_map/extend/pallas_call | solution.py:237
  12.2 0.0 collective-permute-done.1.pack_ref
  12.2 4.7 %finish.1 = (f32[4,4,1024]{2,1,0:T(4,128)S(1)}, f32[4,1,4,1024]{3,2,1,0:T(4,128)}) custom-call(s32[1]{0:T(128)} %bitcast.slot_ref, f32[4,8,128]{2,1,0:T(8,128)S(1)} %get-tuple-element.17.coef_ref, f32[4,4,1024]{2,1,0:T(4,128)S(1)} %get-tuple-element.15.lat_ref, f32[4,4,1024]{2,1,0:T(4,128)S(1)} %get-tuple-element.18.noise_ref, ...), custom_call_target="tpu_custom_call" | custom-call | flops 786432000 | tf_op jit(solution)/shard_map/finish/pallas_call | solution.py:268
  16.9 1.5 %collective-permute-start.2 = (f32[4,4,1024]{2,1,0:T(4,128)S(1)}, f32[4,4,1024]{2,1,0:T(4,128)S(1)}, u32[]{:S(2)}, u32[]{:S(2)}) collective-permute-start(f32[4,4,1024]{2,1,0:T(4,128)S(1)} %get-tuple-element.24), channel_id=1, source_target_pairs={{0,4},{4,0},{8,12},{12,8},{16,20},{20,16},{24,28},{28,24},{1,5},{5... | collective-permute-start | bytes 196616 | tf_op jit(solution)/shard_map/ppermute | solution.py:306
  18.4 2.8 %collective-permute-done.2 = f32[4,4,1024]{2,1,0:T(4,128)S(1)} collective-permute-done((f32[4,4,1024]{2,1,0:T(4,128)S(1)}, f32[4,4,1024]{2,1,0:T(4,128)S(1)}, u32[]{:S(2)}, u32[]{:S(2)}) %collective-permute-start.2) | collective-permute-done | bytes 65568 | tf_op jit(solution)/shard_map/ppermute | solution.py:306
  21.3 0.1 add_bitcast_fusion.2
  21.4 3.7 %collective-permute-start.5 = (f32[1,4,4,1024]{3,2,1,0:T(4,128)S(1)}, f32[1,4,4,1024]{3,2,1,0:T(4,128)S(1)}, u32[]{:S(2)}, u32[]{:S(2)}) collective-permute-start(f32[1,4,4,1024]{3,2,1,0:T(4,128)S(1)} %get-tuple-element.29), channel_id=1, source_target_pairs={{0,24},{4,28},{8,0},{12,4},{16,8},{20,12},{24,16},{28,20},{1,25},{... | collective-permute-start | bytes 196616 | tf_op jit(solution)/shard_map/ppermute | solution.py:324
  25.1 0.0 collective-permute-start.4
  25.1 1.0 %collective-permute-start.3 = (f32[1,4,4,1024]{3,2,1,0:T(4,128)S(1)}, f32[1,4,4,1024]{3,2,1,0:T(4,128)S(1)}, u32[]{:S(2)}, u32[]{:S(2)}) collective-permute-start(f32[1,4,4,1024]{3,2,1,0:T(4,128)S(1)} %get-tuple-element.28), channel_id=1, source_target_pairs={{0,8},{4,12},{8,16},{12,20},{16,24},{20,28},{24,0},{28,4},{1,9},{5... | collective-permute-start | bytes 196616 | tf_op jit(solution)/shard_map/ppermute | solution.py:324
  26.1 1.5 %collective-permute-done.5 = f32[1,4,4,1024]{3,2,1,0:T(4,128)S(1)} collective-permute-done((f32[1,4,4,1024]{3,2,1,0:T(4,128)S(1)}, f32[1,4,4,1024]{3,2,1,0:T(4,128)S(1)}, u32[]{:S(2)}, u32[]{:S(2)}) %collective-permute-start.5) | collective-permute-done | bytes 65568 | tf_op jit(solution)/shard_map/ppermute | solution.py:324
  27.5 3.7 %collective-permute-done.4 = f32[1,4,4,1024]{3,2,1,0:T(4,128)S(1)} collective-permute-done((f32[1,4,4,1024]{3,2,1,0:T(4,128)S(1)}, f32[1,4,4,1024]{3,2,1,0:T(4,128)S(1)}, u32[]{:S(2)}, u32[]{:S(2)}) %collective-permute-start.4) | collective-permute-done | bytes 65568 | tf_op jit(solution)/shard_map/ppermute | solution.py:324
  31.3 0.0 collective-permute-done.3
  31.3 0.1 fusion.1
  31.4 5.8 %all-gather = f32[1,4,4,4096]{3,2,1,0:T(4,128)S(1)} all-gather(f32[1,4,4,1024]{3,2,1,0:T(4,128)S(1)} %fusion.1), channel_id=2, replica_groups=mesh['tm'=8,'mp'=4] {'mp'}, dimensions={3}, use_global_device_ids=true | all-gather | bytes 327680 | tf_op jit(solution)/shard_map/all_gather | solution.py:368
  37.1 0.7 %copy.14 = f32[4,1,4,4096]{3,2,1,0:T(4,128)} copy(f32[4,1,4,4096]{3,2,1,0:T(4,128)S(1)} %bitcast.24) | data formatting | bytes 524288
  (8 shorter events, 0.0 us)
Async XLA Ops:
  0.6 0.7 %copy-start.1 = (f32[320,4]{0,1:T(4,128)S(1)}, f32[320,4]{0,1:T(4,128)}, u32[]{:S(2)}) copy-start(f32[320,4]{0,1:T(4,128)} %param.18) | copy-start | bytes 15364
  0.6 0.7 %copy-start = (f32[4,320]{1,0:T(4,128)S(1)}, f32[4,320]{1,0:T(4,128)}, u32[]{:S(2)}) copy-start(f32[4,320]{1,0:T(4,128)} %in_ref.1) | copy-start | bytes 15364
  0.7 0.7 %copy-start.2 = (s32[4]{0:T(128)S(1)}, s32[4]{0:T(128)}, u32[]{:S(2)}) copy-start(s32[4]{0:T(128)} %start_ref.3) | copy-start | bytes 52
  1.3 5.2 %copy-start.3 = (f32[8,1024]{1,0:T(8,128)S(1)}, f32[8,1024]{1,0:T(8,128)}, u32[]{:S(2)}) copy-start(f32[8,1024]{1,0:T(8,128)} %constant.83.clone.plan_ref) | copy-start | bytes 98308
  3.5 6.3 %collective-permute-start = (f32[1,24,320]{2,1,0:T(8,128)S(1)}, f32[1,24,320]{2,1,0:T(8,128)S(1)}, u32[]{:S(2)}, u32[]{:S(2)}) collective-permute-start(f32[1,24,320]{2,1,0:T(8,128)S(1)} %bitcast.19), channel_id=1, source_target_pairs={{0,2},{1,3},{2,0},{3,1},{4,6},{5,7},{6,4},{7,5},{8,10},{9,11},{10,... | collective-permute-start | bytes 92168 | tf_op jit(solution)/shard_map/ppermute | solution.py:340
  9.8 2.4 %collective-permute-start.1 = (f32[2,24,320]{2,1,0:T(8,128)S(1)}, f32[2,24,320]{2,1,0:T(8,128)S(1)}, u32[]{:S(2)}, u32[]{:S(2)}) collective-permute-start(f32[2,24,320]{2,1,0:T(8,128)S(1)} %pad_maximum_fusion), channel_id=1, source_target_pairs={{0,1},{1,0},{2,3},{3,2},{4,5},{5,4},{6,7},{7,6},{8,9},{9,8},{10,11... | collective-permute-start | bytes 184328 | tf_op jit(solution)/shard_map/ppermute | solution.py:340
  16.9 1.5 %copy-start.4 = (s32[4]{0:T(128)S(1)}, s32[4]{0:T(128)}, u32[]{:S(2)}) copy-start(s32[4]{0:T(128)} %param.13) | copy-start | bytes 52
  16.9 4.4 %collective-permute-start.2 = (f32[4,4,1024]{2,1,0:T(4,128)S(1)}, f32[4,4,1024]{2,1,0:T(4,128)S(1)}, u32[]{:S(2)}, u32[]{:S(2)}) collective-permute-start(f32[4,4,1024]{2,1,0:T(4,128)S(1)} %get-tuple-element.24), channel_id=1, source_target_pairs={{0,4},{4,0},{8,12},{12,8},{16,20},{20,16},{24,28},{28,24},{1,5},{5... | collective-permute-start | bytes 196616 | tf_op jit(solution)/shard_map/ppermute | solution.py:306
  21.4 6.1 %collective-permute-start.5 = (f32[1,4,4,1024]{3,2,1,0:T(4,128)S(1)}, f32[1,4,4,1024]{3,2,1,0:T(4,128)S(1)}, u32[]{:S(2)}, u32[]{:S(2)}) collective-permute-start(f32[1,4,4,1024]{3,2,1,0:T(4,128)S(1)} %get-tuple-element.29), channel_id=1, source_target_pairs={{0,24},{4,28},{8,0},{12,4},{16,8},{20,12},{24,16},{28,20},{1,25},{... | collective-permute-start | bytes 196616 | tf_op jit(solution)/shard_map/ppermute | solution.py:324
  25.1 6.2 %collective-permute-start.4 = (f32[1,4,4,1024]{3,2,1,0:T(4,128)S(1)}, f32[1,4,4,1024]{3,2,1,0:T(4,128)S(1)}, u32[]{:S(2)}, u32[]{:S(2)}) collective-permute-start(f32[1,4,4,1024]{3,2,1,0:T(4,128)S(1)} %get-tuple-element.30), channel_id=1, source_target_pairs={{0,16},{4,20},{8,24},{12,28},{16,0},{20,4},{24,8},{28,12},{1,17},{... | collective-permute-start | bytes 196616 | tf_op jit(solution)/shard_map/ppermute | solution.py:324
  25.1 6.2 %collective-permute-start.3 = (f32[1,4,4,1024]{3,2,1,0:T(4,128)S(1)}, f32[1,4,4,1024]{3,2,1,0:T(4,128)S(1)}, u32[]{:S(2)}, u32[]{:S(2)}) collective-permute-start(f32[1,4,4,1024]{3,2,1,0:T(4,128)S(1)} %get-tuple-element.28), channel_id=1, source_target_pairs={{0,8},{4,12},{8,16},{12,20},{16,24},{20,28},{24,0},{28,4},{1,9},{5... | collective-permute-start | bytes 196616 | tf_op jit(solution)/shard_map/ppermute | solution.py:324
